TPU v7x, 128 devices: a whole 4x4x4 slice. The times are simulated.
128 devices in a mesh: cp: 2 (over core), fsdp: 64 (over z, y, x).
Axes of the slice: x: 4, y: 4, z: 4, core: 2. Of those that a mesh axis runs over, the one named last changes fastest.
Arguments:
- hidden: bfloat16 [64, 1024, 2048], P('fsdp', 'cp')
- tok_pos: int32 [64, 1024], P('fsdp', 'cp')
- grad_out: bfloat16 [64, 1024, 2048], P('fsdp', 'cp')
- norm_gain: float32 [2048], P(('fsdp', 'cp'))
- w_query: bfloat16 [2048, 2048], P(('fsdp', 'cp'))
- w_key: bfloat16 [2048, 256], P(('fsdp', 'cp'))
- w_value: bfloat16 [2048, 256], P(('fsdp', 'cp'))
- w_out: bfloat16 [2048, 2048], P(('fsdp', 'cp'))
Outputs:
- output 1: bfloat16 [64, 1024, 2048], P('fsdp', 'cp')
- output 2: bfloat16 [64, 1024, 2048], P('fsdp', 'cp')
- output 3: float32 [2048, 2048], P(('fsdp', 'cp'))
- output 4: float32 [2048, 256], P(('fsdp', 'cp'))
- output 5: float32 [2048, 256], P(('fsdp', 'cp'))
- output 6: float32 [2048, 2048], P(('fsdp', 'cp'))
- output 7: float32 [2048], P(('fsdp', 'cp'))
All inputs are finite; a program needn't handle non-finite values.
Results may differ from a plain program's by a relative error of at most 0.00684.
Values are sent between devices in bfloat16 or wider.
A program may use at most 1 GiB of HBM per device.

v0:
```python
import functools
import jax
import jax.numpy as jnp
import numpy as np
from jax import lax
from jax.experimental import pallas as pl
from jax.experimental.pallas import tpu as pltpu
from jax.sharding import PartitionSpec as P

HEAD_DIM = 128
ROPE_THETA = 1000000.0
RMS_EPS = 1e-5
SCALE = HEAD_DIM ** -0.5
LOG2E = 1.4426950408889634
COLORS = ((0, 384, 384), (768, 384, 384), (1536, 384, 384))

MESH = pl.DeviceIdType.MESH
AXES = ('x', 'y', 'z')
ORDERS = (('x', 'y', 'z'), ('y', 'z', 'x'), ('z', 'x', 'y'))
ALL = pl.ds(0, 4)


def torus():
    f = lax.axis_index('fsdp')
    return {'x': lax.rem(f, 4), 'y': lax.rem(lax.div(f, 4), 4), 'z': lax.div(f, 16)}


def step(pos, axis, hop):
    return lax.rem(pos[axis] + hop, 4)


class Comm:
    def __init__(self, send_sems, recv_sems, local_sems):
        self.pos = torus()
        self.core = lax.axis_index('cp')
        self.sems = (send_sems, recv_sems, local_sems)
        self.used = self.used_local = 0
        self.sent, self.exchanged, self.stored = [], [], []

    def far(self, axis, hop):
        p = dict(self.pos)
        p[axis] = step(self.pos, axis, hop)
        return {'fsdp': (p['z'] * 4 + p['y']) * 4 + p['x'], 'cp': self.core}

    def peer(self):
        return {'fsdp': lax.axis_index('fsdp'), 'cp': 1 - self.core}

    def barrier(self):
        sem = pltpu.get_barrier_semaphore()
        for axis in AXES:
            for hop in (1, 2, 3):
                pl.semaphore_signal(sem, inc=1, device_id=self.far(axis, hop), device_id_type=MESH)
        pl.semaphore_signal(sem, inc=1, device_id=self.peer(), device_id_type=MESH)
        pl.semaphore_wait(sem, 10)

    def _copy(self, src, dst, device):
        i = self.used
        self.used += 1
        c = pltpu.make_async_remote_copy(src_ref=src, dst_ref=dst, send_sem=self.sems[0].at[i], recv_sem=self.sems[1].at[i], device_id=device, device_id_type=MESH)
        c.start()
        return c

    def send(self, src, dst, device):
        c = self._copy(src, dst, device)
        self.sent.append(c)
        return c

    def trade(self, src, dst):
        self.exchanged.append(self._copy(src, dst, self.peer()))

    def local(self, src, dst):
        i = self.used_local
        self.used_local += 1
        c = pltpu.make_async_copy(src, dst, self.sems[2].at[i])
        c.start()
        return c

    def store(self, src, dst):
        self.stored.append(self.local(src, dst))

    def finish(self):
        for c in self.sent:
            c.wait_send()
        for c in self.exchanged:
            c.wait_send()
            c.wait_recv()
        for c in self.stored:
            c.wait()


def pick(ref, sel, cols):
    return ref.at[sel['z'], sel['y'], sel['x'], :, pl.ds(cols[0], cols[1])]


def sem_scratch(remote, local):
    return [pltpu.SemaphoreType.DMA((remote,)), pltpu.SemaphoreType.DMA((remote,)), pltpu.SemaphoreType.DMA((local,))]


def add_into(dst, *srcs):
    lead = dst.shape[:-2]
    n = 1
    for v in lead:
        n *= v

    def body(i):
        idx, rest = [], i
        for v in reversed(lead):
            idx.append(lax.rem(rest, v))
            rest = lax.div(rest, v)
        idx = tuple(reversed(idx))
        total = dst[idx]
        for s in srcs:
            total = total + s[idx]
        dst[idx] = total

    if n == 1:
        total = dst[...]
        for s in srcs:
            total = total + s[...]
        dst[...] = total
    else:
        pl.loop(0, n)(body)


def scatter_kernel(colors, pieces, *refs):
    n_in = len(pieces)
    grads, gpart = refs[:n_in], refs[n_in]
    out, gout = refs[n_in + 1:n_in + 3]
    part, buf1, buf2, buf3, gpeer, gz, gy, gx, *sems = refs[n_in + 3:]
    comm = Comm(*sems)
    pos, core = comm.pos, comm.core
    loads = [[] for _ in colors]
    for k, (lo, na, nb) in enumerate(colors):
        for ref, start, width in pieces_in(grads, pieces, lo, na + nb):
            src, (at, n) = ref, width
            loads[k].append(comm.local(src.at[:, :, :, :, pl.ds(start, n)], part.at[:, :, :, :, pl.ds(at, n)]))
    comm.barrier()
    gstage = [comm.send(gpart, gpeer, comm.peer())]
    held = [dict(x=ALL, y=ALL, z=ALL) for _ in colors]
    for phase, buf in enumerate((buf1, buf2, buf3)):
        flight = []
        for k, (lo, na, nb) in enumerate(colors):
            d = ORDERS[k][phase]
            a, b = (lo, na), (lo + na, nb)
            if phase == 0:
                for c in loads[k]:
                    c.wait()
            up, dn = comm.far(d, 1), comm.far(d, 3)
            nxt, prv, opp = (dict(held[k], **{d: step(pos, d, hop)}) for hop in (1, 3, 2))
            r2a = comm.send(pick(part, opp, a), buf.at[k, 0], up)
            r2b = comm.send(pick(part, opp, b), buf.at[k, 1], dn)
            n1b = comm.send(pick(part, nxt, b), buf.at[k, 2], up)
            m1a = comm.send(pick(part, prv, a), buf.at[k, 3], dn)
            flight.append([r2a, r2b, n1b, m1a])
        for c in gstage:
            c.wait_recv()
        if phase == 0:
            for j in range(4):
                gz[j] = gpart[j] + gpeer[j]
            gstage = [comm.send(gz.at[step(pos, 'z', hop)], gz.at[3 + hop], comm.far('z', hop)) for hop in (1, 2, 3)]
        elif phase == 1:
            gy[0] = (gz[pos['z']] + gz[4]) + (gz[5] + gz[6])
            gstage = [comm.send(gy.at[0], gy.at[hop], comm.far('y', hop)) for hop in (1, 2, 3)]
        else:
            gx[0] = (gy[0] + gy[1]) + (gy[2] + gy[3])
            gstage = [comm.send(gx.at[0], gx.at[hop], comm.far('x', hop)) for hop in (1, 2, 3)]
        for k, (lo, na, nb) in enumerate(colors):
            d = ORDERS[k][phase]
            a, b = (lo, na), (lo + na, nb)
            nxt, prv = (dict(held[k], **{d: step(pos, d, hop)}) for hop in (1, 3))
            r2a, r2b, n1b, m1a = flight[k]
            r2a.wait_recv()
            add_into(pick(part, nxt, a), buf.at[k, 0])
            n1a = comm.send(pick(part, nxt, a), buf.at[k, 4], comm.far(d, 1))
            r2b.wait_recv()
            add_into(pick(part, prv, b), buf.at[k, 1])
            m1b = comm.send(pick(part, prv, b), buf.at[k, 5], comm.far(d, 3))
            flight[k] += [n1a, m1b]
        for k, (lo, na, nb) in enumerate(colors):
            d = ORDERS[k][phase]
            a, b = (lo, na), (lo + na, nb)
            r2a, r2b, n1b, m1a, n1a, m1b = flight[k]
            held[k] = dict(held[k], **{d: pos[d]})
            m1a.wait_recv()
            n1a.wait_recv()
            add_into(pick(part, held[k], a), buf.at[k, 3], buf.at[k, 4])
            n1b.wait_recv()
            m1b.wait_recv()
            add_into(pick(part, held[k], b), buf.at[k, 2], buf.at[k, 5])
    for c in gstage:
        c.wait_recv()
    gout[...] = (gx[0] + gx[1]) + (gx[2] + gx[3])
    keep = pl.ds(pl.multiple_of(core * 16, 16), 16)
    give = pl.ds(pl.multiple_of((1 - core) * 16, 16), 16)
    chip = part.at[pos['z'], pos['y'], pos['x']]
    comm.trade(chip.at[give], out.at[1])
    comm.store(chip.at[keep], out.at[0])
    comm.finish()


def pieces_in(grads, pieces, lo, n):
    found, at = [], 0
    for ref, width in zip(grads, pieces):
        s, e = max(lo, at), min(lo + n, at + width)
        if s < e:
            found.append((ref, s - at, (s, e - s)))
        at += width
    return found


def reduce_scatter(grads, gpart, colors, collective_id):
    pieces = [g.shape[-1] for g in grads]
    width = sum(pieces)
    half = max(max(a, b) for _, a, b in colors)
    assert all(a == half and b == half for _, a, b in colors)
    any_ = pl.BlockSpec(memory_space=pl.ANY)
    vmem = pl.BlockSpec(memory_space=pltpu.VMEM)
    f32 = jnp.float32
    return pl.pallas_call(
        functools.partial(scatter_kernel, colors, pieces),
        out_shape=[jax.ShapeDtypeStruct((2, 16, width), f32), jax.ShapeDtypeStruct((8, 128), f32)],
        in_specs=[any_] * len(grads) + [vmem],
        out_specs=[any_, vmem],
        scratch_shapes=[pltpu.VMEM((4, 4, 4, 32, width), f32), pltpu.VMEM((3, 6, 4, 4, 32, half), f32), pltpu.VMEM((3, 6, 4, 32, half), f32), pltpu.VMEM((3, 6, 32, half), f32), pltpu.VMEM((4, 8, 128), f32), pltpu.VMEM((7, 8, 128), f32), pltpu.VMEM((4, 8, 128), f32), pltpu.VMEM((4, 8, 128), f32)] + sem_scratch(96, 32),
        compiler_params=pltpu.CompilerParams(collective_id=collective_id, has_side_effects=True, vmem_limit_bytes=60 * 2**20),
        name='scatter_gradients',
    )(*[g.reshape(4, 4, 4, 32, -1) for g in grads], gpart)


QKV_COLORS = ((0, 256, 256), (512, 256, 128), (896, 128, 256))
WO_COLORS = ((0, 128, 128), (256, 128, 256), (640, 256, 128))
ROWS = 512
TOKENS = 1024
DIM = 2048
HALF = 1024
QKV = 1280


def dot(a, b):
    return jnp.dot(a, b, preferred_element_type=jnp.float32)


def dot_nt(a, b):
    return lax.dot_general(a, b, (((1,), (1,)), ((), ())), preferred_element_type=jnp.float32)


def tile_at(i, n):
    return pl.ds(pl.multiple_of(i * n, n), n)


class Gather:
    def __init__(self, comm, ref, colors, land):
        self.comm, self.ref, self.colors, self.land = comm, ref, colors, land
        self.held = [dict(comm.pos) for _ in colors]

    def parts(self, k):
        lo, na, nb = self.colors[k]
        return (lo, na), (lo + na, nb)

    def move(self, s, cols, to):
        return self.comm.send(pick(self.ref, s, cols), pick(self.ref, s, cols), to)

    def begin(self, phase):
        self.phase, self.first, self.second = phase, [], []
        for k in range(3):
            a, b = self.parts(k)
            d = ORDERS[k][phase]
            up, dn, s = self.comm.far(d, 1), self.comm.far(d, 3), self.held[k]
            self.first.append([self.move(s, cols, to) for cols, to in ((a, up), (b, dn), (b, up), (a, dn))])
        if phase == 2:
            for k in range(3):
                for cols in self.parts(k):
                    self.land(self.ref, self.held[k], cols)

    def at(self, k, hop):
        d = ORDERS[k][self.phase]
        return dict(self.held[k], **{d: step(self.comm.pos, d, hop)})

    def forward(self):
        for k in range(3):
            a, b = self.parts(k)
            d = ORDERS[k][self.phase]
            self.first[k][0].wait_recv()
            c = self.move(self.at(k, 3), a, self.comm.far(d, 1))
            self.first[k][1].wait_recv()
            self.second.append((c, self.move(self.at(k, 1), b, self.comm.far(d, 3))))
            if self.phase == 2:
                self.land(self.ref, self.at(k, 3), a)
                self.land(self.ref, self.at(k, 1), b)

    def end(self):
        for k in range(3):
            a, b = self.parts(k)
            d = ORDERS[k][self.phase]
            for c, hop, cols in ((self.first[k][2], 3, b), (self.first[k][3], 1, a), (self.second[k][0], 2, a), (self.second[k][1], 2, b)):
                c.wait_recv()
                if self.phase == 2:
                    self.land(self.ref, self.at(k, hop), cols)
            self.held[k] = dict(self.held[k], **{d: ALL})


def head_kernel(hidden, dy, wq, wk, wv, wo, pos, gtile, cos_t, sin_t,
                qt_o, dot_o, k_o, kt_o, v_o, vt_o, rt_o, dyc_o, wqkv_o, wqkvp_o, wo_o, wop_o, gain_o,
                hid2, dy2, dys, rs, rt, wqkv, wout, wpeer, pi, pos2, qt, dot_s, kk, kt, vv, vt, gain, gbuf, gx, gy, gz, *sems):
    comm = Comm(*sems)
    pos_c, core = comm.pos, comm.core
    bf16, f32 = jnp.bfloat16, jnp.float32
    peer = comm.peer()
    rows = tile_at(core, 16)
    mine_qkv = wqkv.at[pos_c['z'], pos_c['y'], pos_c['x'], rows]
    mine_wo = wout.at[pos_c['z'], pos_c['y'], pos_c['x'], rows]

    def weight_parts(c):
        return ((wq.at[:, tile_at(c, HALF)], mine_qkv.at[:, pl.ds(0, HALF)]), (wk.at[:, tile_at(c, 128)], mine_qkv.at[:, pl.ds(HALF, 128)]),
                (wv.at[:, tile_at(c, 128)], mine_qkv.at[:, pl.ds(HALF + 128, 128)]), (wo.at[:, tile_at(c, HALF)], mine_wo))

    loads = [comm.local(s, d) for s, d in weight_parts(core)]
    load_x = [comm.local(hidden, hid2.at[0]), comm.local(dy, dy2.at[0])]
    comm.barrier()
    swaps = [comm.send(s, d, peer) for s, d in weight_parts(1 - core)]
    gstage = [comm.send(gtile, gbuf, peer)]
    swap_pos = comm.send(pos, pos2.at[1], peer)
    swap_dy = comm.send(dy, dy2.at[1], peer)
    swap_x = comm.send(hidden, hid2.at[1], peer)
    pos2[0] = pos[...]
    for c in loads:
        c.wait()
    gstage[0].wait_recv()
    gx[0] = gtile[...] + gbuf[...]
    gstage = [comm.send(gx.at[0], gx.at[hop], comm.far('x', hop)) for hop in (1, 2, 3)]
    for c in swaps:
        c.wait_recv()

    def land_qkv(ref, s, cols):
        comm.trade(pick(ref, s, cols), pick(wqkvp_o, s, cols))

    arrived = []

    def land_wo(ref, s, cols):
        arrived.append(comm.send(pick(ref, s, cols), pick(wpeer, s, cols), peer))

    g1 = Gather(comm, wqkv, QKV_COLORS, land_qkv)
    g2 = Gather(comm, wout, WO_COLORS, land_wo)
    g1.begin(0)
    g2.begin(0)

    swap_pos.wait_recv()

    @pl.loop(0, TOKENS // 128)
    def _(i):
        want = lax.broadcasted_iota(jnp.int32, (128, ROWS), 0) + i * 128
        for h in range(2):
            have = pos2[h, 0:1, :]
            pi[tile_at(i, 128), h * ROWS:(h + 1) * ROWS] = jnp.where(want == have, 1.0, 0.0).astype(bf16)

    def gain_x():
        for c in gstage:
            c.wait_recv()
        gy[pos_c['y']] = (gx[0] + gx[1]) + (gx[2] + gx[3])
        return [comm.send(gy.at[pos_c['y']], gy.at[pos_c['y']], comm.far('y', hop)) for hop in (1, 2, 3)]

    g1.forward()
    g2.forward()
    gstage = gain_x()
    g1.end()
    g2.end()
    g1.begin(1)
    g2.begin(1)

    def sort(dst, src2, first, last):
        @pl.loop(first, last)
        def _(i):
            r = tile_at(i, 256)

            @pl.loop(0, DIM // 512)
            def _(j):
                c = tile_at(j, 512)
                acc = dot(pi[r, :ROWS], src2[0, :, c]) + dot(pi[r, ROWS:], src2[1, :, c])
                dst[r, c] = acc.astype(bf16)

    load_x[1].wait()
    swap_dy.wait_recv()
    sort(dys, dy2, 0, 1)
    g1.forward()
    g2.forward()
    for c in gstage:
        c.wait_recv()
    for j in range(4):
        gz[pos_c['z'], j] = gy[j]
    gstage = [comm.send(gz.at[pos_c['z']], gz.at[pos_c['z']], comm.far('z', hop)) for hop in (1, 2, 3)]
    g1.end()
    g1.begin(2)
    g2.end()
    sort(dys, dy2, 1, 3)
    for c in gstage:
        c.wait_recv()
    for i in range(4):
        for j in range(4):
            gain[:, (i * 4 + j) * 128:(i * 4 + j + 1) * 128] = gz[i, j]
    comm.store(gain, gain_o)
    load_x[0].wait()
    swap_x.wait_recv()
    for h in range(2):
        @pl.loop(0, ROWS // 32)
        def _(i):
            r = tile_at(i, 32)
            x = hid2[h, r, :].astype(f32)
            inv = lax.rsqrt(jnp.mean(x * x, axis=-1, keepdims=True) + RMS_EPS)
            hid2[h, r, :] = (x * inv * gain[0:1, :]).astype(bf16)
    g1.forward()
    g2.begin(2)
    sort(dys, dy2, 3, 4)
    comm.store(dys.at[:, tile_at(core, HALF)], dyc_o)
    sort(rs, hid2, 0, 4)
    g1.end()
    comm.store(wqkv, wqkv_o)

    w2 = wqkv.reshape(DIM, QKV)

    def project(t, i):
        r = tile_at(i, 256)
        x = dot(rs[r, :], w2[:, tile_at(t, 256)])
        cos, sin = cos_t[:, r], sin_t[:, r]
        cos = jnp.concatenate([cos, cos], axis=0).T
        sin = jnp.concatenate([-sin, sin], axis=0).T
        return r, x, cos, sin

    def rotate(x, cos, sin):
        return x * cos + pltpu.roll(x, 64, 1) * sin

    @pl.loop(0, 4)
    def _(i):
        r, x, cos, sin = project(4, i)
        key, val = rotate(x[:, :128], cos, sin).astype(bf16), x[:, 128:].astype(bf16)
        kk[r, :] = key
        kt[:, r] = key.T
        vv[r, :] = val
        vt[:, r] = val.T

    def queries(first, last):
        @pl.loop(first, last)
        def _(t):
            @pl.loop(0, 4)
            def _(i):
                r, x, cos, sin = project(t, i)
                for h in range(2):
                    q = rotate(x[:, h * 128:(h + 1) * 128], cos, sin).astype(bf16)
                    qt[tile_at(2 * t + h, 128), r] = q.T

    queries(0, 1)
    g2.forward()
    queries(1, 4)
    for src, dst in ((kk, k_o), (kt, kt_o), (vv, v_o), (vt, vt_o), (qt, qt_o)):
        comm.store(src, dst)

    @pl.loop(0, DIM // 256)
    def _(i):
        c = tile_at(i, 256)

        @pl.loop(0, TOKENS // 256)
        def _(j):
            r = tile_at(j, 256)
            rt[c, r] = rs[r, c].T
    comm.store(rt, rt_o)
    g2.end()
    for c in arrived:
        c.wait_recv()
    comm.store(wout, wo_o)
    comm.store(wpeer, wop_o)
    own, other = wout.reshape(DIM, HALF), wpeer.reshape(DIM, HALF)

    @pl.loop(0, HALF // 256)
    def _(i):
        r = pl.ds(pl.multiple_of(core * HALF + i * 256, 256), 256)

        @pl.loop(0, TOKENS // 256)
        def _(j):
            t = tile_at(j, 256)
            acc = dot_nt(own[r, :], dys[t, tile_at(core, HALF)]) + dot_nt(other[r, :], dys[t, tile_at(1 - core, HALF)])
            dot_s[tile_at(i, 256), t] = acc.astype(bf16)
    comm.store(dot_s, dot_o)
    comm.finish()


def head(hidden, dy, wq, wk, wv, wo, pos, gtile, cos_t, sin_t):
    bf16, f32 = jnp.bfloat16, jnp.float32
    any_ = pl.BlockSpec(memory_space=pl.ANY)
    vmem = pl.BlockSpec(memory_space=pltpu.VMEM)
    S = lambda shape, d=bf16: jax.ShapeDtypeStruct(shape, d)
    V = lambda shape, d=bf16: pltpu.VMEM(shape, d)
    w_qkv, w_out = (4, 4, 4, 32, QKV), (4, 4, 4, 32, HALF)
    sq, tall, wide = (HALF, TOKENS), (TOKENS, 128), (128, TOKENS)
    return pl.pallas_call(
        head_kernel,
        out_shape=[S(sq), S(sq), S(tall), S(wide), S(tall), S(wide), S((DIM, TOKENS)), S((TOKENS, HALF)), S(w_qkv), S(w_qkv), S(w_out), S(w_out), S((8, DIM), f32)],
        in_specs=[any_] * 6 + [vmem] * 4,
        out_specs=[any_] * 13,
        scratch_shapes=[V((2, ROWS, DIM)), V((2, ROWS, DIM)), V((TOKENS, DIM)), V((TOKENS, DIM)), V((DIM, TOKENS)), V(w_qkv), V(w_out), V(w_out), V((TOKENS, TOKENS)), V((2, 8, ROWS), jnp.int32),
                        V(sq), V(sq), V(tall), V(wide), V(tall), V(wide), V((8, DIM), f32), V((8, 128), f32), V((4, 8, 128), f32), V((4, 8, 128), f32), V((4, 4, 8, 128), f32)] + sem_scratch(192, 32),
        compiler_params=pltpu.CompilerParams(collective_id=0, has_side_effects=True, vmem_limit_bytes=60 * 2**20),
        name='head',
    )(hidden, dy, wq, wk, wv, wo, pos, gtile, cos_t, sin_t)


NEG_INF = float('-inf')
QB = 256
KC = 256


def attn_kernel(qt, q, k, kt, v, vt, dot_, do, posk, posq, cos, sin, ot, dqt, dk, dv, s_scr, e_scr, p_scr, d_scr):
    head = pl.program_id(0)
    n = qt.shape[1]
    f32, bf16 = jnp.float32, jnp.bfloat16
    half = HEAD_DIM // 2

    @pl.when(head == 0)
    def _():
        dk[...] = jnp.zeros_like(dk)
        dv[...] = jnp.zeros_like(dv)

    def dot(a, b):
        return jnp.dot(a, b, preferred_element_type=f32)

    @pl.loop(0, n // QB)
    def _(j):
        cols = pl.ds(pl.multiple_of(j * QB, QB), QB)
        q_t, do_t = qt[:, cols], dot_[:, cols]
        q_pos = posq[0:1, cols]
        top = jnp.full((8, QB), NEG_INF, f32)
        for c in range(n // KC):
            rows = slice(c * KC, (c + 1) * KC)
            s = dot(k[rows, :], q_t)
            pk = posk[rows, :]
            vis = jnp.concatenate([pk] * (QB // 128), axis=1) <= q_pos
            s = jnp.where(vis, s, NEG_INF)
            s_scr[rows, :] = s
            top = jnp.maximum(top, jnp.max(s.reshape(KC // 8, 8, QB), axis=0))
        m = jnp.max(top, axis=0, keepdims=True)
        tot = jnp.zeros((8, QB), f32)
        for c in range(n // KC):
            rows = slice(c * KC, (c + 1) * KC)
            e = jnp.exp2((s_scr[rows, :] - m) * (SCALE * LOG2E))
            s_scr[rows, :] = e
            e_scr[rows, :] = e.astype(bf16)
            tot = tot + jnp.sum(e.reshape(KC // 8, 8, QB), axis=0)
        den = jnp.sum(tot, axis=0, keepdims=True)
        inv = 1.0 / den
        o = (dot(vt[...], e_scr[...]) / den).astype(bf16)
        ot[:, cols] = o
        delta = jnp.sum(do_t.astype(f32) * o.astype(f32), axis=0, keepdims=True)
        q_n, do_n = q[cols, :], do[cols, :]
        for c in range(n // KC):
            rows = slice(c * KC, (c + 1) * KC)
            p = s_scr[rows, :] * inv
            dp = dot(v[rows, :], do_t)
            p_scr[rows, :] = p.astype(bf16)
            d_scr[rows, :] = (p * (dp - delta)).astype(bf16)
            dv[rows, :] += dot(p_scr[rows, :], do_n)
            dk[rows, :] += dot(d_scr[rows, :], q_n)
        g = dot(kt[...], d_scr[...]) * SCALE
        co, si = cos[:, cols], sin[:, cols]
        a, b = g[:half], g[half:]
        dqt[:half, cols] = (a * co + b * si).astype(bf16)
        dqt[half:, cols] = (b * co - a * si).astype(bf16)


def attention(qt, q, k, kt, v, vt, dot_, do, posk, posq, cos_t, sin_t):
    heads, n = qt.shape[0] // HEAD_DIM, qt.shape[1]
    by_row = pl.BlockSpec((HEAD_DIM, n), lambda h: (h, 0))
    by_col = pl.BlockSpec((n, HEAD_DIM), lambda h: (0, h))
    whole = lambda a: pl.BlockSpec(a.shape, lambda h: (0, 0))
    f32, bf16 = jnp.float32, jnp.bfloat16
    return pl.pallas_call(
        attn_kernel,
        grid=(heads,),
        in_specs=[by_row, by_col, whole(k), whole(kt), whole(v), whole(vt), by_row, by_col, whole(posk), whole(posq), whole(cos_t), whole(sin_t)],
        out_specs=[by_row, by_row, pl.BlockSpec((n, HEAD_DIM), lambda h: (0, 0)), pl.BlockSpec((n, HEAD_DIM), lambda h: (0, 0))],
        out_shape=[jax.ShapeDtypeStruct((heads * HEAD_DIM, n), bf16), jax.ShapeDtypeStruct((heads * HEAD_DIM, n), bf16), jax.ShapeDtypeStruct((n, HEAD_DIM), f32), jax.ShapeDtypeStruct((n, HEAD_DIM), f32)],
        scratch_shapes=[pltpu.VMEM((n, QB), f32), pltpu.VMEM((n, QB), bf16), pltpu.VMEM((n, QB), bf16), pltpu.VMEM((n, QB), bf16)],
        compiler_params=pltpu.CompilerParams(dimension_semantics=('arbitrary',), vmem_limit_bytes=48 * 2**20),
        cost_estimate=pl.CostEstimate(flops=12 * heads * n * n * HEAD_DIM, bytes_accessed=16 * n * n, transcendentals=heads * n * n),
        name='attention',
    )(qt, q, k, kt, v, vt, dot_, do, posk, posq, cos_t, sin_t)


def rope_tables():
    j = np.arange(HEAD_DIM // 2, dtype=np.float64) / (HEAD_DIM // 2)
    freq = (ROPE_THETA ** -j).astype(np.float32)
    angle = freq[:, None] * np.arange(TOKENS, dtype=np.float32)[None, :]
    return np.cos(angle.astype(np.float64)).astype(np.float32), np.sin(angle.astype(np.float64)).astype(np.float32)


def unrope(x, cos, sin):
    a, b = x[:, :64], x[:, 64:]
    return jnp.concatenate([a * cos + b * sin, b * cos - a * sin], axis=1)


NT = (((1,), (1,)), ((), ()))
TN = (((0,), (0,)), ((), ()))


def solution(mesh):
    def swap(a):
        return lax.ppermute(a, 'cp', [(0, 1), (1, 0)])

    def shard_fn(hidden, tok_pos, grad_out, norm_gain, w_query, w_key, w_value, w_out):
        f32, bf16 = jnp.float32, jnp.bfloat16
        f, core = lax.axis_index('fsdp'), lax.axis_index('cp')
        x, y = lax.rem(f, 4), lax.rem(lax.div(f, 4), 4)
        first = core == 0
        hidden, grad_out = hidden[0], grad_out[0]
        dim, half, rows = DIM, HALF, ROWS

        def order(own, other, axis):
            return jnp.where(first, jnp.concatenate([own, other], axis), jnp.concatenate([other, own], axis))

        cos_t, sin_t = (jnp.asarray(t) for t in rope_tables())
        lane = jnp.arange(128) // 16
        gtile = jnp.broadcast_to(jnp.where(lane == x * 2 + core, jnp.tile(norm_gain, 8), 0.0), (8, 128))
        pos8 = jnp.broadcast_to(tok_pos, (8, rows))
        qt, do_t, k, kt, v, vt, rt, dyc, wqkv, wqkvp, wo_own, wo_peer, gain = head(hidden, grad_out, w_query, w_key, w_value, w_out, pos8, gtile, cos_t, sin_t)
        wqkv, wqkvp = wqkv.reshape(dim, QKV), wqkvp.reshape(dim, QKV)
        gain = gain[0:1]
        ip = jnp.arange(TOKENS)
        posk = jnp.broadcast_to(ip[:, None], (TOKENS, 128))
        posq = jnp.broadcast_to(ip[None, :], (8, TOKENS))
        ot, dqt, dk, dv = attention(qt, qt.T, k, kt, v, vt, do_t, do_t.T, posk, posq, cos_t, sin_t)
        dk = unrope(dk * SCALE, cos_t.T, sin_t.T).astype(bf16)
        dkv = jnp.concatenate([dk, dv.astype(bf16)], axis=1)
        dqkv = jnp.concatenate([dqt.T, dkv], axis=1)
        ot_peer = swap(ot)
        dqkv_peer = swap(dqkv)
        pick_own = (tok_pos[0][:, None] == ip[None, :]).astype(bf16)
        o_t = order(ot, ot_peer, 0)
        o_rows = lax.dot_general(pick_own, o_t, NT, preferred_element_type=f32).astype(bf16)
        wo = order(wo_own.reshape(dim, half), wo_peer.reshape(dim, half), 1)
        xf = hidden.astype(f32)
        result = (xf + jnp.dot(o_rows, wo, preferred_element_type=f32)).astype(bf16)
        grad_o = jnp.dot(o_t, dyc, preferred_element_type=f32)
        grad_qkv = jnp.dot(rt, dqkv, preferred_element_type=f32)
        own_rows = jnp.dot(pick_own, jnp.concatenate([dqkv, dqkv_peer], axis=1), preferred_element_type=f32).astype(bf16)
        dr = lax.dot_general(own_rows[:, :QKV], wqkv, NT, preferred_element_type=f32) + lax.dot_general(own_rows[:, QKV:], wqkvp, NT, preferred_element_type=f32)
        inv = lax.rsqrt(jnp.mean(xf * xf, axis=-1, keepdims=True) + RMS_EPS)
        unit = xf * inv
        drg = dr * gain
        grad_hidden = (grad_out.astype(f32) + inv * (drg - unit * jnp.mean(drg * unit, axis=-1, keepdims=True))).astype(bf16)
        gpart = jnp.pad(jnp.sum(dr * unit, axis=0).reshape(4, 4, 128), ((0, 0), (0, 4), (0, 0)))
        out, gout = reduce_scatter([grad_qkv, grad_o], gpart, COLORS, 1)
        own, other = out[0], out[1]
        cut = lambda a, b: order(own[:, a:b], other[:, a:b], 1)
        grad_gain = lax.dynamic_slice(gout, (y, x * 32 + core * 16), (1, 16)).reshape(16)
        return result[None], grad_hidden[None], cut(0, half), cut(half, half + 128), cut(half + 128, half + 256), cut(half + 256, 2 * half + 256), grad_gain

    row_spec, pos_spec = P('fsdp', 'cp', None), P('fsdp', 'cp')
    weight_spec, gain_spec = P(('fsdp', 'cp'), None), P(('fsdp', 'cp'))
    return jax.shard_map(shard_fn, mesh=mesh, in_specs=(row_spec, pos_spec, row_spec, gain_spec, weight_spec, weight_spec, weight_spec, weight_spec), out_specs=(row_spec, row_spec, weight_spec, weight_spec, weight_spec, weight_spec, gain_spec), check_vma=False)
```

profile of v0, /device:TPU:1, one launch (start us, length us, event | category | flops | bytes accessed | tf_op | source)
XLA Modules:
  0.0 306.8 jit_solution(6897629503906015471)
XLA Ops:
  0.6 0.7 tile.4
  1.3 0.1 tile.10
  1.4 1.3 broadcast_in_dim.16.pos
  2.7 0.6 broadcast_in_dim.18.gtile
  3.3 76.3 %head.1 = (bf16[1024,1024]{1,0:T(8,128)(2,1)}, bf16[1024,1024]{1,0:T(8,128)(2,1)}, bf16[1024,128]{1,0:T(8,128)(2,1)}, bf16[128,1024]{1,0:T(8,128)(2,1)}, bf16[10...) custom-call(bf16[512,2048]{1,0:T(8,128)(2,1)} %bitcast.36, ...), custom_call_target="tpu_custom_call" | custom-call | tf_op jit(solution)/shard_map/head/pallas_call | solution.py:493
  79.6 0.0 copy-start
  79.6 0.0 copy-start.1
  79.7 4.1 %copy.25 = bf16[1024,1024]{0,1:T(8,128)(2,1)} copy(bf16[1024,1024]{1,0:T(8,128)(2,1)} %get-tuple-element.26.qt) | data formatting | bytes 4194304 | tf_op jit(solution)/shard_map/head/pallas_call | solution.py:493
  83.7 2.5 copy.26
  86.3 0.0 copy-done
  86.3 0.0 copy-done.1
  86.4 0.0 copy-done.2
  86.4 0.0 copy-start.3
  86.4 0.9 copy-done.3
  87.3 0.9 copy-done.4
  88.3 0.9 copy-done.5
  89.2 51.6 %attention.1 = (bf16[1024,1024]{1,0:T(8,128)(2,1)S(1)}, bf16[1024,1024]{1,0:T(8,128)(2,1)}, f32[1024,128]{1,0:T(8,128)S(1)}, f32[1024,128]{1,0:T(8,128)S(1)}) custom-call(bf16[1024,1024]{1,0:T(8,128)(2,1)} %get-tuple-element.26.qt, bf16[1024,1024]{1,0:T(8,128)(2,1)} %bitcast.42, bf16[1024,128]{1,0:T(8,128)(2,1)S(1)} %copy-done.2, ...), custom_call_target="tpu_custom_call" | custom-call | flops 12884901888 | bytes 16777216 | tf_op jit(solution)/shard_map/attention/pallas_call | solution.py:573
  140.8 0.0 collective-permute-start
  140.9 0.3 subtract_convert_fusion
  141.2 0.1 copy.32
  141.3 0.1 copy.33
  141.5 0.1 copy.34
  141.6 3.0 pad_maximum_fusion
  144.6 0.5 collective-permute-start.1
  145.2 1.5 constant_dynamic-update-slice_fusion.4
  146.6 0.8 slice.49
  147.5 0.7 constant_dynamic-update-slice_fusion.3
  148.1 0.7 constant_dynamic-update-slice_fusion.2
  148.8 0.7 constant_dynamic-update-slice_fusion.1
  149.5 2.1 fusion.17
  151.6 10.7 %fusion.30 = f32[2048,1280]{1,0:T(8,128)} fusion(bf16[2048,1024]{1,0:T(8,128)(2,1)} %get-tuple-element.41, bf16[1024,128]{0,1:T(8,128)(2,1)S(1)} %copy.34, bf16[1024,64]{0,1:T(8,128)(2,1)S(1)} %copy.33, bf16[1024,64]{0,1:T(8,128)(2,1)S(1)} %copy.32, bf16[1024,1024]{0,1:T(8,128)(2,1)} %bitcast.39), kind=kOutput, calls=%fused_computation.60 | convolution fusion | flops 5379194880 | bytes 17301504 | tf_op jit(solution)/shard_map/dot_general | solution.py:640
  162.4 0.0 collective-permute-done
  162.4 10.1 %fusion.26 = f32[2048,1024]{1,0:T(8,128)} fusion(bf16[1024,1024]{1,0:T(8,128)(2,1)S(1)} %copy-done.12, bf16[1024,1024]{1,0:T(8,128)(2,1)} %collective-permute-done, bf16[1024,1024]{1,0:T(8,128)(2,1)S(1)} %get-tuple-element.32, pred[]{:T(512)S(6)} %eq.28), kind=kOutput, calls=%fused_computation.35 | convolution fusion | flops 4313841664 | bytes 14680065 | tf_op jit(solution)/shard_map/dot_general | solution.py:639
  172.5 18.9 %fusion.18 = bf16[1,512,2048]{2,1,0:T(8,128)(2,1)} fusion(bf16[2048,1024]{1,0:T(8,128)(2,1)} %bitcast.57, bf16[2048,1024]{1,0:T(8,128)(2,1)} %bitcast.56, pred[]{:T(512)S(6)} %eq.28, s32[512]{0:T(512)S(1)} %bitcast.48, bf16[1024,1024]{1,0:T(8,128)(2,1)} %collective-permute-done, bf16[1024,1024]{1,0:T(8,128)(2,1)S(1)} %get-tuple-element.32, ...), kind=kOutput, calls=%fused_computation.26 | convolution fusion | flops 6503792640 | bytes 16779264 | tf_op jit(solution)/shard_map/dot_general | solution.py:638
  191.4 0.0 collective-permute-done.1
  191.4 3.6 %constant_dynamic-update-slice_fusion = bf16[1024,2560]{0,1:T(8,128)(2,1)} fusion(bf16[1024,2560]{0,1:T(8,128)(2,1)} %constant_dynamic-update-slice_fusion.1, bf16[1024,1280]{0,1:T(8,128)(2,1)} %collective-permute-done.1), kind=kLoop, calls=%fused_computation.45 | loop fusion | bytes 5242880 | tf_op jit(solution)/shard_map/concatenate | solution.py:641
  195.0 5.8 %convolution_convert_fusion = bf16[512,2560]{1,0:T(8,128)(2,1)S(1)} fusion(bf16[1024,2560]{0,1:T(8,128)(2,1)} %constant_dynamic-update-slice_fusion, s32[512]{0:T(512)S(1)} %bitcast.49), kind=kOutput, calls=%fused_computation.14 | convolution fusion | flops 2686189568 | bytes 7866368 | tf_op jit(solution)/shard_map/dot_general | solution.py:641
  200.9 0.0 copy-start.6
  200.9 0.0 slice-start.1
  200.9 2.9 fusion.21
  203.8 5.0 %fusion.15 = (f32[2048]{0:T(1024)S(1)}, f32[512]{0:T(512)S(1)}, f32[512,2048]{1,0:T(8,128)}) fusion(f32[512]{0:T(512)S(1)} %add_rsqrt_fusion, bf16[1,512,2048]{2,1,0:T(8,128)(2,1)S(1)} %copy-done.6, f32[2048]{0:T(1024)S(1)} %bitcast.44, f32[512,2048]{1,0:T(8,128)S(1)} %fusion.21, bf16[2048,1280]{1,0:T(8,128)(2,1)S(1)} %bitcast.52, ...), kind=kOutput, calls=%fused_computation.20 | convolution fusion | flops 2692740608 | bytes 17059840 | tf_op jit(solution)/shard_map/dot_general | solution.py:642
  208.9 0.6 pad.4.refs_2_
  209.5 88.1 %scatter_gradients.1 = (f32[2,16,2304]{2,1,0:T(8,128)}, f32[8,128]{1,0:T(8,128)}) custom-call(f32[4,4,4,32,1280]{4,3,2,1,0:T(8,128)} %bitcast.37, f32[4,4,4,32,1024]{4,3,2,1,0:T(8,128)} %bitcast.40, f32[4,8,128]{2,1,0:T(8,128)} %pad.4.refs_2_), custom_call_target="tpu_custom_call" | custom-call | tf_op jit(solution)/shard_map/scatter_gradients/pallas_call | solution.py:219
  297.6 1.0 slice_bitcast_fusion.1
  298.7 5.5 %fusion.19 = bf16[1,512,2048]{2,1,0:T(8,128)(2,1)} fusion(f32[512,2048]{1,0:T(8,128)} %get-tuple-element.59, f32[512]{0:T(512)S(1)} %broadcast_multiply_fusion.1, f32[2048]{0:T(1024)S(1)} %bitcast.45, f32[512]{0:T(512)S(1)} %add_rsqrt_fusion, bf16[1,512,2048]{2,1,0:T(8,128)(2,1)} %param.12, bf16[1,512,2048]{2,1,0:T(8,128)(2,1)S(1)} %copy-done.6), kind=kLoop, calls=%fused_computation.28 | loop fusion | flops 9437184 | bytes 10498048 | tf_op jit(solution)/shard_map/broadcast_in_dim | solution.py:652
  304.2 1.3 dynamic-slice_bitcast_fusion
  305.5 0.7 maximum_select_fusion.10
  306.2 0.6 maximum_select_fusion.12
  (36 shorter events, 0.2 us)
Async XLA Ops:
  79.6 4.1 %copy-start.8 = (bf16[1024,1024]{1,0:T(8,128)(2,1)S(1)}, bf16[1024,1024]{1,0:T(8,128)(2,1)}, u32[]{:S(2)}) copy-start(bf16[1024,1024]{1,0:T(8,128)(2,1)} %get-tuple-element.31.dot_) | copy-start | bytes 6291460
  79.6 6.7 %copy-start = (f32[64,1024]{1,0:T(8,128)S(1)}, f32[64,1024]{1,0:T(8,128)}, u32[]{:S(2)}) copy-start(f32[64,1024]{1,0:T(8,128)} %constant.60.clone.cos_t.cos) | copy-start | bytes 786436
  79.6 6.7 %copy-start.1 = (f32[64,1024]{1,0:T(8,128)S(1)}, f32[64,1024]{1,0:T(8,128)}, u32[]{:S(2)}) copy-start(f32[64,1024]{1,0:T(8,128)} %constant.61.clone.sin_t.sin) | copy-start | bytes 786436
  79.6 6.7 %copy-start.2 = (bf16[1024,128]{1,0:T(8,128)(2,1)S(1)}, bf16[1024,128]{1,0:T(8,128)(2,1)}, u32[]{:S(2)}) copy-start(bf16[1024,128]{1,0:T(8,128)(2,1)} %get-tuple-element.27.k) | copy-start | bytes 786436
  86.4 1.0 copy-start.3
  87.3 0.9 copy-start.4
  88.3 0.9 copy-start.5
  89.2 51.7 %copy-start.9 = (f32[1024,64]{1,0:T(8,128)S(1)}, f32[1024,64]{1,0:T(8,128)}, u32[]{:S(2)}) copy-start(f32[1024,64]{1,0:T(8,128)} %constant.73) | copy-start | bytes 786436
  89.2 51.7 %copy-start.10 = (f32[1024,64]{1,0:T(8,128)S(1)}, f32[1024,64]{1,0:T(8,128)}, u32[]{:S(2)}) copy-start(f32[1024,64]{1,0:T(8,128)} %constant.74) | copy-start | bytes 786436
  140.8 21.5 %collective-permute-start = (bf16[1024,1024]{1,0:T(8,128)(2,1)S(1)}, bf16[1024,1024]{1,0:T(8,128)(2,1)}, u32[]{:S(2)}, u32[]{:S(2)}) collective-permute-start(bf16[1024,1024]{1,0:T(8,128)(2,1)S(1)} %get-tuple-element.32), channel_id=1, source_target_pairs={{0,64},{64,0},{1,65},{65,1},{2,66},{66,2},{3,67},{67,3},{4,68},{68... | collective-permute-start | bytes 6291464 | tf_op jit(solution)/shard_map/ppermute | solution.py:604
  141.6 3.5 %copy-start.7 = (bf16[1024,1024]{1,0:T(8,128)(2,1)S(1)}, bf16[1024,1024]{1,0:T(8,128)(2,1)}, u32[]{:S(2)}) copy-start(bf16[1024,1024]{1,0:T(8,128)(2,1)} %get-tuple-element.35) | copy-start | bytes 6291460
  144.6 46.7 %collective-permute-start.1 = (bf16[1024,1280]{0,1:T(8,128)(2,1)}, bf16[1024,1280]{0,1:T(8,128)(2,1)}, u32[]{:S(2)}, u32[]{:S(2)}) collective-permute-start(bf16[1024,1280]{0,1:T(8,128)(2,1)} %pad_maximum_fusion), channel_id=1, source_target_pairs={{0,64},{64,0},{1,65},{65,1},{2,66},{66,2},{3,67},{67,3},{4,68},{68... | collective-permute-start | bytes 7864328 | tf_op jit(solution)/shard_map/ppermute | solution.py:604
  151.6 10.8 %copy-start.12 = (bf16[1024,1024]{1,0:T(8,128)(2,1)S(1)}, bf16[1024,1024]{1,0:T(8,128)(2,1)}, u32[]{:S(2)}) copy-start(bf16[1024,1024]{1,0:T(8,128)(2,1)} %get-tuple-element.42) | copy-start | bytes 6291460
  162.4 10.1 %copy-start.11 = (s32[1,512]{1,0:T(1,128)S(1)}, s32[1,512]{1,0:T(1,128)}, u32[]{:S(2)}) copy-start(s32[1,512]{1,0:T(1,128)} %param.11) | copy-start | bytes 6148
  191.4 9.5 %slice-start.2 = ((s8[5242880]{0:T(1024)(128)(4,1)}), s8[4194304]{0:T(1024)(128)(4,1)S(1)}, s32[]{:S(2)}) async-start(s8[5242880]{0:T(1024)(128)(4,1)} %bitcast.53), calls=%async_computation.2 | async-start | bytes 8388608
  195.0 5.8 %slice-start.3 = ((s8[5242880]{0:T(1024)(128)(4,1)}), s8[1048576]{0:T(1024)(128)(4,1)S(1)}, s32[]{:S(2)}) async-start(s8[5242880]{0:T(1024)(128)(4,1)} %bitcast.53), calls=%async_computation.3 | async-start | bytes 2097152
  195.0 8.8 %slice-start = ((s8[5242880]{0:T(1024)(128)(4,1)}), s8[4194304]{0:T(1024)(128)(4,1)S(1)}, s32[]{:S(2)}) async-start(s8[5242880]{0:T(1024)(128)(4,1)} %bitcast.50), calls=%async_computation | async-start | bytes 8388608
  200.9 2.9 copy-start.6
  200.9 2.9 slice-start.1
where the time goes:
time: 307 us
  Pallas kernels  216 us (70%)
  matrix products  53.5 us (17%)
  local copies, waits for them, and re-layouts  23.5 us (8%)
  other arithmetic  12.3 us (4%)
    pallas_call x1, Pallas kernels, reduce_scatter(): pl.pallas_call(functools.partial(scatter_kernel, colors, pieces), out_sha...  88.1 us
    pallas_call x1, Pallas kernels, head(): pl.pallas_call(head_kernel, out_shape=[S(sq), S(sq), S(tall), S(wide), S(...  76.3 us
    pallas_call x1, Pallas kernels, attention(): pl.pallas_call(attn_kernel, grid=(heads,), in_specs=[by_row, by_col, whol...  51.6 us
    dot_general x1, matrix products, shard_fn(): result = (xf + jnp.dot(o_rows, wo, preferred_element_type=f32)).astype(bf16)  18.9 us
    dot_general x1, matrix products, shard_fn(): grad_qkv = jnp.dot(rt, dqkv, preferred_element_type=f32)  10.7 us
    dot_general x1, matrix products, shard_fn(): grad_o = jnp.dot(o_t, dyc, preferred_element_type=f32)  10.1 us
    pallas_call x2, local copies, waits for them, and re-layouts, head(): pl.pallas_call(head_kernel, out_shape=[S(sq), S(sq), S(tall), S(wide), S(...  6.63 us
    unnamed x38, local copies, waits for them, and re-layouts  6.44 us
  transfers between devices with their start and end apart: 2, of which 0 were waited for; matrix products, arithmetic and copies ran while one was open for 16% of the time, Pallas kernels for 0%

commit v1 on v0

v1 whole, which is shorter than its diff:
```python
import functools
import jax
import jax.numpy as jnp
import numpy as np
from jax import lax
from jax.experimental import pallas as pl
from jax.experimental.pallas import tpu as pltpu
from jax.sharding import PartitionSpec as P

LANES, SUBS, RING, TRIO = 128, 8, 4, 3
PAIR, ROWS, CHIP, SHARE = 256, 512, 32, 16
HEAD_DIM = LANES
ROPE_THETA = 1000000.0
RMS_EPS = 1e-5
SCALE = HEAD_DIM ** -0.5
LOG2E = 1.4426950408889634

MESH = pl.DeviceIdType.MESH
AXES = ('x', 'y', 'z')
ORDERS = (('x', 'y', 'z'), ('y', 'z', 'x'), ('z', 'x', 'y'))
ALL = pl.ds(0, RING)


def torus():
    f = lax.axis_index('fsdp')
    return {'x': lax.rem(f, RING), 'y': lax.rem(lax.div(f, RING), RING), 'z': lax.div(f, SHARE)}


def step(pos, axis, hop):
    return lax.rem(pos[axis] + hop, RING)


class Comm:
    def __init__(self, send_sems, recv_sems, local_sems):
        self.pos = torus()
        self.core = lax.axis_index('cp')
        self.sems = (send_sems, recv_sems, local_sems)
        self.used = self.used_local = 0
        self.sent, self.exchanged, self.stored = [], [], []

    def far(self, axis, hop):
        p = dict(self.pos)
        p[axis] = step(self.pos, axis, hop)
        return {'fsdp': (p['z'] * RING + p['y']) * RING + p['x'], 'cp': self.core}

    def peer(self):
        return {'fsdp': lax.axis_index('fsdp'), 'cp': 1 - self.core}

    def barrier(self):
        sem = pltpu.get_barrier_semaphore()
        for axis in AXES:
            for hop in (1, 2, TRIO):
                pl.semaphore_signal(sem, inc=1, device_id=self.far(axis, hop), device_id_type=MESH)
        pl.semaphore_signal(sem, inc=1, device_id=self.peer(), device_id_type=MESH)
        pl.semaphore_wait(sem, 10)

    def _copy(self, src, dst, device):
        i = self.used
        self.used += 1
        c = pltpu.make_async_remote_copy(src_ref=src, dst_ref=dst, send_sem=self.sems[0].at[i], recv_sem=self.sems[1].at[i], device_id=device, device_id_type=MESH)
        c.start()
        return c

    def send(self, src, dst, device):
        c = self._copy(src, dst, device)
        self.sent.append(c)
        return c

    def trade(self, src, dst):
        self.exchanged.append(self._copy(src, dst, self.peer()))

    def local(self, src, dst):
        i = self.used_local
        self.used_local += 1
        c = pltpu.make_async_copy(src, dst, self.sems[2].at[i])
        c.start()
        return c

    def store(self, src, dst):
        self.stored.append(self.local(src, dst))

    def finish(self):
        for c in self.sent:
            c.wait_send()
        for c in self.exchanged:
            c.wait_send()
            c.wait_recv()
        for c in self.stored:
            c.wait()


def pick(ref, sel, cols):
    return ref.at[sel['z'], sel['y'], sel['x'], :, pl.ds(cols[0], cols[1])]


def sem_scratch(remote, local):
    return [pltpu.SemaphoreType.DMA((remote,)), pltpu.SemaphoreType.DMA((remote,)), pltpu.SemaphoreType.DMA((local,))]


def add_into(dst, *srcs):
    lead = dst.shape[:-2]
    n = 1
    for v in lead:
        n *= v

    def body(i):
        idx, rest = [], i
        for v in reversed(lead):
            idx.append(lax.rem(rest, v))
            rest = lax.div(rest, v)
        idx = tuple(reversed(idx))
        total = dst[idx]
        for s in srcs:
            total = total + s[idx]
        dst[idx] = total

    if n == 1:
        total = dst[...]
        for s in srcs:
            total = total + s[...]
        dst[...] = total
    else:
        pl.loop(0, n)(body)


QKV_COLORS = ((0, PAIR, PAIR), (ROWS, PAIR, LANES), (896, LANES, PAIR))
WO_COLORS = ((0, LANES, LANES), (PAIR, LANES, PAIR), (640, PAIR, LANES))
TOKENS = 1024
DIM = 2048
HALF = 1024
QKV = 1280


def dot(a, b):
    return jnp.dot(a, b, preferred_element_type=jnp.float32)


def dot_nt(a, b):
    return lax.dot_general(a, b, (((1,), (1,)), ((), ())), preferred_element_type=jnp.float32)


def tile_at(i, n):
    return pl.ds(pl.multiple_of(i * n, n), n)


class Gather:
    def __init__(self, comm, ref, colors, land):
        self.comm, self.ref, self.colors, self.land = comm, ref, colors, land
        self.held = [dict(comm.pos) for _ in colors]

    def parts(self, k):
        lo, na, nb = self.colors[k]
        return (lo, na), (lo + na, nb)

    def move(self, s, cols, to):
        return self.comm.send(pick(self.ref, s, cols), pick(self.ref, s, cols), to)

    def begin(self, phase):
        self.phase, self.first, self.second = phase, [], []
        for k in range(TRIO):
            a, b = self.parts(k)
            d = ORDERS[k][phase]
            up, dn, s = self.comm.far(d, 1), self.comm.far(d, TRIO), self.held[k]
            self.first.append([self.move(s, cols, to) for cols, to in ((a, up), (b, dn), (b, up), (a, dn))])
        if phase == 2:
            for k in range(TRIO):
                for cols in self.parts(k):
                    self.land(self.ref, self.held[k], cols)

    def at(self, k, hop):
        d = ORDERS[k][self.phase]
        return dict(self.held[k], **{d: step(self.comm.pos, d, hop)})

    def forward(self):
        for k in range(TRIO):
            a, b = self.parts(k)
            d = ORDERS[k][self.phase]
            self.first[k][0].wait_recv()
            c = self.move(self.at(k, TRIO), a, self.comm.far(d, 1))
            self.first[k][1].wait_recv()
            self.second.append((c, self.move(self.at(k, 1), b, self.comm.far(d, TRIO))))
            if self.phase == 2:
                self.land(self.ref, self.at(k, TRIO), a)
                self.land(self.ref, self.at(k, 1), b)

    def end(self):
        for k in range(TRIO):
            a, b = self.parts(k)
            d = ORDERS[k][self.phase]
            for c, hop, cols in ((self.first[k][2], TRIO, b), (self.first[k][TRIO], 1, a), (self.second[k][0], 2, a), (self.second[k][1], 2, b)):
                c.wait_recv()
                if self.phase == 2:
                    self.land(self.ref, self.at(k, hop), cols)
            self.held[k] = dict(self.held[k], **{d: ALL})


def head_kernel(hidden, dy, wq, wk, wv, wo, pos, gtile, cos_t, sin_t,
                qt_o, dot_o, k_o, kt_o, v_o, vt_o, rt_o, dyc_o, wqkv_o, wqkvp_o, wo_o, wop_o, gain_o,
                hid2, dy2, dys, rs, rt, wqkv, wout, wpeer, pi, pos2, qt, dot_s, kk, kt, vv, vt, gain, gbuf, gx, gy, gz, *sems):
    comm = Comm(*sems)
    pos_c, core = comm.pos, comm.core
    bf16, f32 = jnp.bfloat16, jnp.float32
    peer = comm.peer()
    rows = tile_at(core, SHARE)
    mine_qkv = wqkv.at[pos_c['z'], pos_c['y'], pos_c['x'], rows]
    mine_wo = wout.at[pos_c['z'], pos_c['y'], pos_c['x'], rows]

    def weight_parts(c):
        return ((wq.at[:, tile_at(c, HALF)], mine_qkv.at[:, pl.ds(0, HALF)]), (wk.at[:, tile_at(c, LANES)], mine_qkv.at[:, pl.ds(HALF, LANES)]),
                (wv.at[:, tile_at(c, LANES)], mine_qkv.at[:, pl.ds(HALF + LANES, LANES)]), (wo.at[:, tile_at(c, HALF)], mine_wo))

    loads = [comm.local(s, d) for s, d in weight_parts(core)]
    load_x = [comm.local(hidden, hid2.at[0]), comm.local(dy, dy2.at[0])]
    comm.barrier()
    swaps = [comm.send(s, d, peer) for s, d in weight_parts(1 - core)]
    gstage = [comm.send(gtile, gbuf, peer)]
    swap_pos = comm.send(pos, pos2.at[1], peer)
    swap_dy = comm.send(dy, dy2.at[1], peer)
    swap_x = comm.send(hidden, hid2.at[1], peer)
    pos2[0] = pos[...]
    for c in loads:
        c.wait()
    gstage[0].wait_recv()
    gx[0] = gtile[...] + gbuf[...]
    gstage = [comm.send(gx.at[0], gx.at[hop], comm.far('x', hop)) for hop in (1, 2, TRIO)]
    for c in swaps:
        c.wait_recv()

    def land_qkv(ref, s, cols):
        comm.trade(pick(ref, s, cols), pick(wqkvp_o, s, cols))

    arrived = []

    def land_wo(ref, s, cols):
        arrived.append(comm.send(pick(ref, s, cols), pick(wpeer, s, cols), peer))

    g1 = Gather(comm, wqkv, QKV_COLORS, land_qkv)
    g2 = Gather(comm, wout, WO_COLORS, land_wo)
    g1.begin(0)
    g2.begin(0)

    swap_pos.wait_recv()

    @pl.loop(0, TOKENS // LANES)
    def _(i):
        want = lax.broadcasted_iota(jnp.int32, (LANES, ROWS), 0) + i * LANES
        for h in range(2):
            have = pos2[h, 0:1, :]
            pi[tile_at(i, LANES), h * ROWS:(h + 1) * ROWS] = jnp.where(want == have, 1.0, 0.0).astype(bf16)

    def gain_x():
        for c in gstage:
            c.wait_recv()
        gy[pos_c['y']] = (gx[0] + gx[1]) + (gx[2] + gx[TRIO])
        return [comm.send(gy.at[pos_c['y']], gy.at[pos_c['y']], comm.far('y', hop)) for hop in (1, 2, TRIO)]

    g1.forward()
    g2.forward()
    gstage = gain_x()
    g1.end()
    g2.end()
    g1.begin(1)
    g2.begin(1)

    def sort(dst, src2, first, last):
        @pl.loop(first, last)
        def _(i):
            r = tile_at(i, PAIR)

            @pl.loop(0, DIM // ROWS)
            def _(j):
                c = tile_at(j, ROWS)
                acc = dot(pi[r, :ROWS], src2[0, :, c]) + dot(pi[r, ROWS:], src2[1, :, c])
                dst[r, c] = acc.astype(bf16)

    load_x[1].wait()
    swap_dy.wait_recv()
    sort(dys, dy2, 0, 1)
    g1.forward()
    g2.forward()
    for c in gstage:
        c.wait_recv()
    for j in range(RING):
        gz[pos_c['z'], j] = gy[j]
    gstage = [comm.send(gz.at[pos_c['z']], gz.at[pos_c['z']], comm.far('z', hop)) for hop in (1, 2, TRIO)]
    g1.end()
    g1.begin(2)
    g2.end()
    sort(dys, dy2, 1, TRIO)
    for c in gstage:
        c.wait_recv()
    for i in range(RING):
        for j in range(RING):
            gain[:, (i * RING + j) * LANES:(i * RING + j + 1) * LANES] = gz[i, j]
    comm.store(gain, gain_o)
    load_x[0].wait()
    swap_x.wait_recv()
    for h in range(2):
        @pl.loop(0, ROWS // CHIP)
        def _(i):
            r = tile_at(i, CHIP)
            x = hid2[h, r, :].astype(f32)
            inv = lax.rsqrt(jnp.mean(x * x, axis=-1, keepdims=True) + RMS_EPS)
            hid2[h, r, :] = (x * inv * gain[0:1, :]).astype(bf16)
    g1.forward()
    g2.begin(2)
    sort(dys, dy2, TRIO, RING)
    comm.store(dys.at[:, tile_at(core, HALF)], dyc_o)
    sort(rs, hid2, 0, RING)
    g1.end()
    comm.store(wqkv, wqkv_o)

    w2 = wqkv.reshape(DIM, QKV)

    def project(t, i):
        r = tile_at(i, PAIR)
        x = dot(rs[r, :], w2[:, tile_at(t, PAIR)])
        cos, sin = cos_t[:, r], sin_t[:, r]
        cos = jnp.concatenate([cos, cos], axis=0).T
        sin = jnp.concatenate([-sin, sin], axis=0).T
        return r, x, cos, sin

    def rotate(x, cos, sin):
        return x * cos + pltpu.roll(x, 64, 1) * sin

    @pl.loop(0, RING)
    def _(i):
        r, x, cos, sin = project(RING, i)
        key, val = rotate(x[:, :LANES], cos, sin).astype(bf16), x[:, LANES:].astype(bf16)
        kk[r, :] = key
        kt[:, r] = key.T
        vv[r, :] = val
        vt[:, r] = val.T

    def queries(first, last):
        @pl.loop(first, last)
        def _(t):
            @pl.loop(0, RING)
            def _(i):
                r, x, cos, sin = project(t, i)
                for h in range(2):
                    q = rotate(x[:, h * LANES:(h + 1) * LANES], cos, sin).astype(bf16)
                    qt[tile_at(2 * t + h, LANES), r] = q.T

    queries(0, 1)
    g2.forward()
    queries(1, RING)
    for src, dst in ((kk, k_o), (kt, kt_o), (vv, v_o), (vt, vt_o), (qt, qt_o)):
        comm.store(src, dst)

    @pl.loop(0, DIM // PAIR)
    def _(i):
        c = tile_at(i, PAIR)

        @pl.loop(0, TOKENS // PAIR)
        def _(j):
            r = tile_at(j, PAIR)
            rt[c, r] = rs[r, c].T
    comm.store(rt, rt_o)
    g2.end()
    for c in arrived:
        c.wait_recv()
    comm.store(wout, wo_o)
    comm.store(wpeer, wop_o)
    own, other = wout.reshape(DIM, HALF), wpeer.reshape(DIM, HALF)

    @pl.loop(0, HALF // PAIR)
    def _(i):
        r = pl.ds(pl.multiple_of(core * HALF + i * PAIR, PAIR), PAIR)

        @pl.loop(0, TOKENS // PAIR)
        def _(j):
            t = tile_at(j, PAIR)
            acc = dot_nt(own[r, :], dys[t, tile_at(core, HALF)]) + dot_nt(other[r, :], dys[t, tile_at(1 - core, HALF)])
            dot_s[tile_at(i, PAIR), t] = acc.astype(bf16)
    comm.store(dot_s, dot_o)
    comm.finish()


def head(hidden, dy, wq, wk, wv, wo, pos, gtile, cos_t, sin_t):
    bf16, f32 = jnp.bfloat16, jnp.float32
    any_ = pl.BlockSpec(memory_space=pl.ANY)
    vmem = pl.BlockSpec(memory_space=pltpu.VMEM)
    S = lambda shape, d=bf16: jax.ShapeDtypeStruct(shape, d)
    V = lambda shape, d=bf16: pltpu.VMEM(shape, d)
    w_qkv, w_out = (RING, RING, RING, CHIP, QKV), (RING, RING, RING, CHIP, HALF)
    sq, tall, wide = (HALF, TOKENS), (TOKENS, LANES), (LANES, TOKENS)
    return pl.pallas_call(
        head_kernel,
        out_shape=[S(sq), S(sq), S(tall), S(wide), S(tall), S(wide), S((DIM, TOKENS)), S((TOKENS, HALF)), S(w_qkv), S(w_qkv), S(w_out), S(w_out), S((SUBS, DIM), f32)],
        in_specs=[any_] * 6 + [vmem] * RING,
        out_specs=[any_] * 13,
        scratch_shapes=[V((2, ROWS, DIM)), V((2, ROWS, DIM)), V((TOKENS, DIM)), V((TOKENS, DIM)), V((DIM, TOKENS)), V(w_qkv), V(w_out), V(w_out), V((TOKENS, TOKENS)), V((2, SUBS, ROWS), jnp.int32),
                        V(sq), V(sq), V(tall), V(wide), V(tall), V(wide), V((SUBS, DIM), f32), V((SUBS, LANES), f32), V((RING, SUBS, LANES), f32), V((RING, SUBS, LANES), f32), V((RING, RING, SUBS, LANES), f32)] + sem_scratch(192, CHIP),
        compiler_params=pltpu.CompilerParams(collective_id=0, has_side_effects=True, vmem_limit_bytes=60 * 2**20),
        name='head',
    )(hidden, dy, wq, wk, wv, wo, pos, gtile, cos_t, sin_t)


HEADS = SUBS
QB = PAIR
NBLK = TOKENS // QB
UNIT_Q = tuple(range(HEADS))
UNIT_K, UNIT_V = SUBS, 9
UNIT_O = tuple(range(10, 18))
N_UNITS = 18
LINES = ((0, TRIO, 6, 9, 12, 15), (1, RING, 7, 10, 13, SHARE), (2, 5, SUBS, 11, 14, 17))
COLOR = {u: k for k, line in enumerate(LINES) for u in line}
SLOT = {u: i % RING for line in LINES for i, u in enumerate(line)}
PLACE = {**{u: u for u in range(12)}, **{u: u - 12 for u in range(12, 18)}}
LAG = (0, RING, SUBS, 10, 12, 13, 14)
HALVES = (pl.ds(0, SHARE), pl.ds(SHARE, SHARE))


class Scatter:
    def __init__(self, comm, part, bufs, fin, out, send_sems, recv_sems, swap_sems):
        self.pos, self.part, self.bufs, self.fin, self.out = comm.pos, part, bufs, fin, out
        self.sems, self.swap_sems = (send_sems, recv_sems), swap_sems
        self.near = {(a, hop): comm.far(a, hop) for a in AXES for hop in (1, TRIO)}
        self.hops = {(a, hop): step(comm.pos, a, hop) for a in AXES for hop in (1, 2, TRIO)}
        self.peer, self.core = comm.peer(), comm.core
        self.keep, self.give = tile_at(comm.core, SHARE), tile_at(1 - comm.core, SHARE)

    def sel(self, u, phase, hop):
        order = ORDERS[COLOR[u]]
        s = {a: ALL for a in AXES}
        for a in order[:phase]:
            s[a] = self.pos[a]
        a = order[phase]
        s[a] = self.hops[a, hop] if hop else self.pos[a]
        return s

    def view(self, u, phase, hop, half):
        s = self.sel(u, phase, hop)
        return self.part.at[PLACE[u], s['z'], s['y'], s['x'], HALVES[half], :]

    def buf(self, u, phase, name):
        return self.bufs[phase].at[COLOR[u], SLOT[u], name]

    def copy(self, u, phase, name):
        hop, half, to = ((2, 0, 1), (2, 1, TRIO), (1, 1, 1), (TRIO, 0, TRIO), (1, 0, 1), (TRIO, 1, TRIO))[name]
        i = (u * TRIO + phase) * 6 + name
        return pltpu.make_async_remote_copy(src_ref=self.view(u, phase, hop, half), dst_ref=self.buf(u, phase, name), send_sem=self.sems[0].at[i], recv_sem=self.sems[1].at[i],
                                            device_id=self.near[ORDERS[COLOR[u]][phase], to], device_id_type=MESH)

    def launch(self, u, phase):
        for name in range(RING):
            self.copy(u, phase, name).start()

    def swap(self, u):
        cols = pl.ds(u * LANES, LANES)
        give = pltpu.make_async_remote_copy(src_ref=self.fin.at[u, self.give], dst_ref=self.out.at[1, :, cols], send_sem=self.swap_sems.at[u], recv_sem=self.swap_sems.at[N_UNITS + u], device_id=self.peer, device_id_type=MESH)
        keep = pltpu.make_async_copy(self.fin.at[u, self.keep], self.out.at[0, :, cols], self.swap_sems.at[2 * N_UNITS + u])
        return give, keep

    def run(self, u, stage):
        if stage == 0:
            return self.launch(u, 0)
        phase = (stage - 1) // 2
        if stage % 2:
            for first, hop, half, then in ((0, 1, 0, RING), (1, TRIO, 1, 5)):
                self.copy(u, phase, first).wait_recv()
                add_into(self.view(u, phase, hop, half), self.buf(u, phase, first))
                self.copy(u, phase, then).start()
            return
        for half, names in ((0, (TRIO, RING)), (1, (2, 5))):
            for name in names:
                self.copy(u, phase, name).wait_recv()
            srcs = [self.buf(u, phase, name) for name in names]
            if phase < 2:
                add_into(self.view(u, phase, 0, half), *srcs)
            else:
                self.fin[u, HALVES[half], :] = self.view(u, phase, 0, half)[...] + (srcs[0][...] + srcs[1][...])
        if phase < 2:
            return self.launch(u, phase + 1)
        for c in self.swap(u):
            c.start()

    def drain_sends(self, u):
        for phase in range(TRIO):
            for name in range(6):
                self.copy(u, phase, name).wait_send()

    def finish(self, u):
        give, keep = self.swap(u)
        give.wait_send()
        give.wait_recv()
        keep.wait()


def attend(head, qt, do_t, k, kt, v, vt, cos, sin, o_rows, ot, dq, dk, dv, s_scr, e_scr, p_scr, d_scr, between):
    f32, bf16 = jnp.float32, jnp.bfloat16
    mine = tile_at(head, LANES)
    below = lax.broadcasted_iota(jnp.int32, (QB, QB), 0) <= lax.broadcasted_iota(jnp.int32, (QB, QB), 1)

    def fold(x, op):
        return op(x.reshape(-1, SUBS, QB), axis=0)

    def scores(j):
        cols, b = slice(j * QB, (j + 1) * QB), j % 2
        q_t = qt[mine, cols]
        top = None
        for c in range(j + 1):
            rows = slice(c * QB, (c + 1) * QB)
            s = dot(k[rows, :], q_t)
            if c == j:
                s = jnp.where(below, s, -jnp.inf)
            s_scr[b, rows, :] = s
            t = fold(s, jnp.max)
            top = t if top is None else jnp.maximum(top, t)
        return jnp.max(top, axis=0, keepdims=True)

    def rest(j, m):
        cols, b, n = slice(j * QB, (j + 1) * QB), j % 2, (j + 1) * QB
        q_t, d_t = qt[mine, cols], do_t[mine, cols]
        tot = None
        for c in range(j + 1):
            rows = slice(c * QB, (c + 1) * QB)
            e = jnp.exp2((s_scr[b, rows, :] - m) * (SCALE * LOG2E))
            s_scr[b, rows, :] = e
            e_scr[b, rows, :] = e.astype(bf16)
            t = fold(e, jnp.sum)
            tot = t if tot is None else tot + t
        den = jnp.sum(tot, axis=0, keepdims=True)
        inv = 1.0 / den
        o = (dot(vt[:, :n], e_scr[b, :n, :]) / den).astype(bf16)
        ot[o_rows, cols] = o
        delta = jnp.sum(d_t.astype(f32) * o.astype(f32), axis=0, keepdims=True)
        for c in range(j + 1):
            rows = slice(c * QB, (c + 1) * QB)
            p = s_scr[b, rows, :] * inv
            p_scr[b, rows, :] = p.astype(bf16)
            d_scr[b, rows, :] = (p * (dot(v[rows, :], d_t) - delta)).astype(bf16)
        dv[:n, :] += dot_nt(p_scr[b, :n, :], d_t)
        dk[:n, :] += dot_nt(d_scr[b, :n, :], q_t)
        g = dot(kt[:, :n], d_scr[b, :n, :]) * SCALE
        co, si = cos[:, cols], sin[:, cols]
        x, y = g[:64], g[64:]
        dq[tile_at(head, LANES), cols] = jnp.concatenate([x * co + y * si, y * co - x * si], axis=0).astype(bf16)

    m = scores(0)
    for j in range(NBLK):
        later = scores(j + 1) if j + 1 < NBLK else None
        rest(j, m)
        m = later
        if j == 2:
            between()


def tail_kernel(qt, do_t, k, kt, v, vt, rt, dyc, wqkv, wqkvp, wo, wop, gain, hidden, dy, pos_col, cos, sin,
                result, grad_x, out, gout,
                a1, a2, ks, kts, vs, vts, rts, ots, dqo, dqp, dkvo, dkvp, dk, dv, s_scr, e_scr, p_scr, d_scr, dycs, part, buf1, buf2, buf3, fin, pick_rows, onat, dnat, xs, wkv, wkvp, drs, gacc, gpart, gpeer, gz, gy, gx,
                send_sems, recv_sems, swap_sems, trade_send, trade_recv, local_sems):
    comm = Comm(trade_send, trade_recv, local_sems)
    comm.used = 2 * HEADS
    f32, bf16 = jnp.float32, jnp.bfloat16
    core, peer = comm.core, comm.peer()
    sc = Scatter(comm, part, (buf1, buf2, buf3), fin, out, send_sems, recv_sems, swap_sems)
    loads = [comm.local(s, d) for s, d in ((qt, a1), (do_t, a2), (k, ks), (kt, kts), (v, vs), (vt, vts))]
    load_r = comm.local(rt, rts)
    later = [comm.local(s, d) for s, d in ((dyc, dycs), (hidden, xs), (wqkv.at[:, pl.ds(HALF, PAIR)], wkv), (wqkvp.at[:, pl.ds(HALF, PAIR)], wkvp))]
    comm.barrier()
    dk[...] = jnp.zeros_like(dk)
    dv[...] = jnp.zeros_like(dv)

    @pl.loop(0, ROWS // LANES)
    def _(i):
        have = pos_col[tile_at(i, LANES), :]
        for c in range(TOKENS // LANES):
            want = lax.broadcasted_iota(jnp.int32, (LANES, LANES), 1) + c * LANES
            pick_rows[tile_at(i, LANES), c * LANES:(c + 1) * LANES] = jnp.where(want == have, 1.0, 0.0).astype(bf16)

    for c in loads:
        c.wait()

    events = {}
    clock = [0]

    def schedule(u, at):
        for stage, lag in enumerate(LAG):
            events.setdefault(at + lag, []).append((stage, u))

    for h in range(HEADS):
        schedule(h, 2 * h + 1)

    def tick(t):
        for stage, u in sorted(events.pop(t, []), reverse=True):
            sc.run(u, stage)

    def head_trades(h):
        row = tile_at(core * HEADS + h, LANES)
        mine = tile_at(h, LANES)
        return [pltpu.make_async_remote_copy(src_ref=s, dst_ref=d, send_sem=trade_send.at[i], recv_sem=trade_recv.at[i], device_id=peer, device_id_type=MESH)
                for s, d, i in ((ots.at[row], ots.at[row], h), (dqo.at[mine], dqp.at[mine], HEADS + h))]

    def gradient(place, left, right, mul):
        @pl.loop(0, RING)
        def _(z):
            g = mul(left[tile_at(z, ROWS), :], right)
            n = g.shape[1] // LANES
            for i in range(n):
                part[place + i, z] = g[:, i * LANES:(i + 1) * LANES].reshape(RING, RING, CHIP, LANES)

    load_r.wait()
    tick(0)

    @pl.loop(0, HEADS)
    def _(h):
        def between():
            for hh in range(1, HEADS):
                if events.get(2 * hh):
                    pl.when(h == hh)(functools.partial(tick, 2 * hh))

        attend(h, a1, a2, ks, kts, vs, vts, cos, sin, tile_at(core * HEADS + h, LANES), ots, dqo, dk, dv, s_scr, e_scr, p_scr, d_scr, between)
        for c in head_trades(h):
            c.start()

        @pl.loop(0, RING)
        def _(z):
            g = dot_nt(rts[tile_at(z, ROWS), :], dqo[tile_at(h, LANES), :])
            part[h, z] = g.reshape(RING, RING, CHIP, LANES)
        for hh in range(HEADS):
            pl.when(h == hh)(functools.partial(tick, 2 * hh + 1))

    t = [2 * HEADS]

    def beat():
        tick(t[0])
        t[0] += 1

    key = dk[...] * SCALE
    co, si = jnp.concatenate([cos[...], cos[...]], axis=0).T, jnp.concatenate([sin[...], -sin[...]], axis=0).T
    dkvo[:, :LANES] = (key * co + pltpu.roll(key, 64, 1) * si).astype(bf16)
    dkvo[:, LANES:] = dv[...].astype(bf16)
    comm.trade(dkvo, dkvp)
    gradient(UNIT_K, rts, dkvo[...], dot)
    schedule(UNIT_K, t[0])
    schedule(UNIT_V, t[0])
    beat()
    wo_loads = [comm.local(wo.at[tile_at(i, HALF)], a) for i, a in ((0, a1), (1, a2))]
    wq_load = comm.local(wqkv.at[:, pl.ds(0, HALF)], rts)
    for c in later:
        c.wait()
    for h in range(HEADS):
        for c in head_trades(h):
            c.wait()

    def output_gradient(i):
        for u in (10 + 2 * i, 11 + 2 * i):
            if PLACE[u] != u:
                sc.drain_sends(PLACE[u])
        gradient(PLACE[10 + 2 * i], ots, dycs[:, i * PAIR:(i + 1) * PAIR], dot)
        for u in (10 + 2 * i, 11 + 2 * i):
            schedule(u, t[0])

    def natural(dst, src_t, n):
        @pl.loop(0, n // PAIR)
        def _(i):
            dst[:, tile_at(i, PAIR)] = dot_nt(pick_rows[...], src_t[tile_at(i, PAIR), :]).astype(bf16)

    def project_out(col, weights):
        @pl.loop(0, HALF // PAIR)
        def _(i):
            c = tile_at(i, PAIR)
            dst = pl.ds(pl.multiple_of(col + i * PAIR, PAIR), PAIR)
            acc = dot(onat[:, :HALF], weights[0][:, c]) + dot(onat[:, HALF:], weights[1][:, c])
            dnat[:, dst] = (xs[:, dst].astype(f32) + acc).astype(bf16)

    output_gradient(0)
    beat()
    natural(onat, ots, DIM)
    beat()
    output_gradient(1)
    beat()
    for c in wo_loads:
        c.wait()
    project_out(core * HALF, (a1, a2))
    beat()
    beat()
    wo_loads = [comm.local(wop.at[tile_at(i, HALF)], a) for i, a in ((0, a1), (1, a2))]
    output_gradient(2)
    beat()
    for c in wo_loads:
        c.wait()
    project_out((1 - core) * HALF, (a1, a2))
    beat()
    beat()
    save = comm.local(dnat.at[:, pl.ds(0, DIM)], result)
    load_dy = comm.local(dy, onat)
    beat()
    output_gradient(TRIO)
    beat()
    wqp_load = comm.local(wqkvp.at[:, pl.ds(0, HALF)], ots)
    save.wait()
    for c in comm.exchanged:
        c.wait_recv()
    natural(dnat, dqo, HALF)
    beat()
    for i, src in ((2 * HALF, dkvo), (2 * HALF + PAIR, dkvp)):
        dnat[:, i:i + PAIR] = dot(pick_rows[...], src[...]).astype(bf16)

    @pl.loop(0, HALF // PAIR)
    def _(i):
        dnat[:, pl.ds(pl.multiple_of(HALF + i * PAIR, PAIR), PAIR)] = dot_nt(pick_rows[...], dqp[tile_at(i, PAIR), :]).astype(bf16)
    beat()
    wq_load.wait()
    wqp_load.wait()
    load_dy.wait()
    gacc[...] = jnp.zeros_like(gacc)

    def back(i):
        r = pl.ds(i * LANES, LANES)

        @pl.loop(0, DIM // PAIR)
        def _(j):
            c = tile_at(j, PAIR)
            acc = dot_nt(dnat[r, :HALF], rts[c, :]) + dot_nt(dnat[r, HALF:2 * HALF], ots[c, :])
            acc = acc + dot_nt(dnat[r, 2 * HALF:2 * HALF + PAIR], wkv[c, :]) + dot_nt(dnat[r, 2 * HALF + PAIR:], wkvp[c, :])
            drs[:, c] = acc

        @pl.loop(0, LANES // SHARE)
        def _(j):
            q = pl.ds(pl.multiple_of(i * LANES + j * SHARE, SHARE), SHARE)
            x, d = xs[q, :].astype(f32), drs[tile_at(j, SHARE), :]
            inv = lax.rsqrt(jnp.mean(x * x, axis=-1, keepdims=True) + RMS_EPS)
            unit = x * inv
            gacc[...] += jnp.sum((d * unit).reshape(2, SUBS, DIM), axis=0)
            dg = d * gain[0:1, :]
            onat[q, :] = (onat[q, :].astype(f32) + inv * (dg - unit * jnp.mean(dg * unit, axis=-1, keepdims=True))).astype(bf16)

    for i in range(RING):
        back(i)
        beat()
    comm.store(onat, grad_x)
    total = jnp.sum(gacc[...], axis=0, keepdims=True)
    gpart[...] = jnp.zeros_like(gpart)
    for i in range(RING):
        for j in range(RING):
            gpart[i, j:j + 1, :] = total[:, (i * RING + j) * LANES:(i * RING + j + 1) * LANES]
    stage = [comm.send(gpart, gpeer, peer)]
    beat()
    for c in stage:
        c.wait_recv()
    for j in range(RING):
        gz[j] = gpart[j] + gpeer[j]
    stage = [comm.send(gz.at[step(comm.pos, 'z', hop)], gz.at[TRIO + hop], comm.far('z', hop)) for hop in (1, 2, TRIO)]
    beat()
    for c in stage:
        c.wait_recv()
    gy[0] = (gz[comm.pos['z']] + gz[RING]) + (gz[5] + gz[6])
    stage = [comm.send(gy.at[0], gy.at[hop], comm.far('y', hop)) for hop in (1, 2, TRIO)]
    beat()
    for c in stage:
        c.wait_recv()
    gx[0] = (gy[0] + gy[1]) + (gy[2] + gy[TRIO])
    stage = [comm.send(gx.at[0], gx.at[hop], comm.far('x', hop)) for hop in (1, 2, TRIO)]
    while events:
        beat()
    for c in stage:
        c.wait_recv()
    gout[...] = (gx[0] + gx[1]) + (gx[2] + gx[TRIO])
    for u in range(N_UNITS):
        sc.finish(u)
    for u in range(6, N_UNITS):
        sc.drain_sends(u)
    for c in comm.sent + comm.exchanged:
        c.wait_send()
    for c in comm.stored:
        c.wait()


def tail(qt, do_t, k, kt, v, vt, rt, dyc, wqkv, wqkvp, wo, wop, gain, hidden, dy, pos_col, cos, sin):
    bf16, f32 = jnp.bfloat16, jnp.float32
    any_ = pl.BlockSpec(memory_space=pl.ANY)
    vmem = pl.BlockSpec(memory_space=pltpu.VMEM)
    S = lambda shape, d=bf16: jax.ShapeDtypeStruct(shape, d)
    V = lambda shape, d=bf16: pltpu.VMEM(shape, d)
    D = lambda n: pltpu.SemaphoreType.DMA((n,))
    sq, tall, wide = (HALF, TOKENS), (TOKENS, LANES), (LANES, TOKENS)
    own = (ROWS, DIM)
    return pl.pallas_call(
        tail_kernel,
        out_shape=[S(own), S(own), S((2, SHARE, N_UNITS * LANES), f32), S((SUBS, LANES), f32)],
        in_specs=[any_] * 12 + [vmem] + [any_] * 2 + [vmem] * TRIO,
        out_specs=[any_] * TRIO + [vmem],
        scratch_shapes=[V(sq), V(sq), V(tall), V(wide), V(tall), V(wide), V((DIM, TOKENS)), V((DIM, TOKENS)), V(sq), V(sq), V((TOKENS, PAIR)), V((TOKENS, PAIR)), V(tall, f32), V(tall, f32),
                        V((2, TOKENS, QB), f32), V((2, TOKENS, QB)), V((2, TOKENS, QB)), V((2, TOKENS, QB)), V(sq), V((12, RING, RING, RING, CHIP, LANES), f32),
                        V((TRIO, RING, 6, RING, RING, SHARE, LANES), f32), V((TRIO, RING, 6, RING, SHARE, LANES), f32), V((TRIO, RING, 6, SHARE, LANES), f32), V((N_UNITS, CHIP, LANES), f32), V((ROWS, TOKENS)), V(own), V((ROWS, 2 * QKV)), V(own),
                        V((DIM, PAIR)), V((DIM, PAIR)), V((LANES, DIM), f32), V((SUBS, DIM), f32), V((RING, SUBS, LANES), f32), V((RING, SUBS, LANES), f32), V((7, SUBS, LANES), f32), V((RING, SUBS, LANES), f32), V((RING, SUBS, LANES), f32),
                        D(N_UNITS * 18), D(N_UNITS * 18), D(TRIO * N_UNITS), D(2 * HEADS + SHARE), D(2 * HEADS + SHARE), D(CHIP)],
        compiler_params=pltpu.CompilerParams(collective_id=1, has_side_effects=True, vmem_limit_bytes=67043328),
        name='tail',
    )(qt, do_t, k, kt, v, vt, rt, dyc, wqkv, wqkvp, wo, wop, gain, hidden, dy, pos_col, cos, sin)


def rope_tables():
    j = np.arange(HEAD_DIM // 2, dtype=np.float64) / (HEAD_DIM // 2)
    freq = (ROPE_THETA ** -j).astype(np.float32)
    angle = freq[:, None] * np.arange(TOKENS, dtype=np.float32)[None, :]
    return np.cos(angle.astype(np.float64)).astype(np.float32), np.sin(angle.astype(np.float64)).astype(np.float32)


def solution(mesh):
    def shard_fn(hidden, tok_pos, grad_out, norm_gain, w_query, w_key, w_value, w_out):
        f, core = lax.axis_index('fsdp'), lax.axis_index('cp')
        x, y = lax.rem(f, RING), lax.rem(lax.div(f, RING), RING)
        hidden, grad_out = hidden[0], grad_out[0]
        cos_t, sin_t = (jnp.asarray(t) for t in rope_tables())
        lane = jnp.arange(LANES) // SHARE
        gtile = jnp.broadcast_to(jnp.where(lane == x * 2 + core, jnp.tile(norm_gain, SUBS), 0.0), (SUBS, LANES))
        pos8 = jnp.broadcast_to(tok_pos, (SUBS, ROWS))
        pos_col = jnp.broadcast_to(tok_pos[0][:, None], (ROWS, LANES))
        *parts, wqkv, wqkvp, wo, wop, gain = head(hidden, grad_out, w_query, w_key, w_value, w_out, pos8, gtile, cos_t, sin_t)
        result, grad_hidden, out, gout = tail(*parts, wqkv.reshape(DIM, QKV), wqkvp.reshape(DIM, QKV), wo.reshape(DIM, HALF), wop.reshape(DIM, HALF), gain, hidden, grad_out, pos_col, cos_t, sin_t)
        own, other = out[0], out[1]

        def cut(a, b):
            a, b = own[:, a:b], other[:, a:b]
            return jnp.where(core == 0, jnp.concatenate([a, b], 1), jnp.concatenate([b, a], 1))

        grad_gain = lax.dynamic_slice(gout, (y, x * CHIP + core * SHARE), (1, SHARE)).reshape(SHARE)
        return result[None], grad_hidden[None], cut(0, HALF), cut(HALF, HALF + LANES), cut(HALF + LANES, QKV), cut(QKV, QKV + HALF), grad_gain

    row_spec, pos_spec = P('fsdp', 'cp', None), P('fsdp', 'cp')
    weight_spec, gain_spec = P(('fsdp', 'cp'), None), P(('fsdp', 'cp'))
    return jax.shard_map(shard_fn, mesh=mesh, in_specs=(row_spec, pos_spec, row_spec, gain_spec, weight_spec, weight_spec, weight_spec, weight_spec), out_specs=(row_spec, row_spec, weight_spec, weight_spec, weight_spec, weight_spec, gain_spec), check_vma=False)
```

time: 307 us -> 244 us (0.79)
  matrix products: 53.5 us -> 0 us
  Pallas kernels: 216 us -> 229 us
  local copies, waits for them, and re-layouts: 23.5 us -> 11.1 us
  other arithmetic: 12.3 us -> 2.56 us
    dot_general x6 -> x0, matrix products: 53.5 us -> none  [the longest x1 18.9 us: shard_fn(): result = (xf + jnp.dot(o_rows, wo, preferred_element_type=f32)).astype(bf16)]
    pallas_call x2 -> x1, Pallas kernels: 140 us -> 153 us  [tail(): pl.pallas_call(tail_kernel, out_shape=[S(own), S(own), S((2, SHARE, N_UNI...]
    pallas_call x2 -> x0, local copies, waits for them, and re-layouts: 6.63 us -> none  [head(): pl.pallas_call(head_kernel, out_shape=[S(sq), S(sq), S(tall), S(wide), S(...]
    broadcast_in_dim x1 -> x0, other arithmetic: 5.52 us -> none  [shard_fn(): grad_hidden[None]]
    concatenate x1 -> x0, local copies, waits for them, and re-layouts: 3.61 us -> none  [shard_fn(): jnp.concatenate([dqkv, dqkv_peer], axis=1)]
    unnamed x38 -> x4, local copies, waits for them, and re-layouts: 6.44 us -> 4.63 us
  transfers between devices with their start and end apart: 2 -> 0, of which waited for: 0 -> 0; matrix products, arithmetic and copies ran while one was open for 16% -> 0% of each run, Pallas kernels for 0% -> 0%
where the time goes in v1:
time: 244 us
  Pallas kernels  229 us (94%)
  local copies, waits for them, and re-layouts  11.1 us (5%)
  other arithmetic  2.56 us (1%)
    pallas_call x1, Pallas kernels, tail(): pl.pallas_call(tail_kernel, out_shape=[S(own), S(own), S((2, SHARE, N_UNI...  153 us
    pallas_call x1, Pallas kernels, head(): pl.pallas_call(head_kernel, out_shape=[S(sq), S(sq), S(tall), S(wide), S(...  76.4 us

profile of v1, /device:TPU:1, one launch (start us, length us, event | category | flops | bytes accessed | tf_op | source)
XLA Modules:
  0.0 243.5 jit_solution(3750647937937118843)
XLA Ops:
  0.7 0.7 tile.4
  1.3 0.1 tile.10
  1.4 0.6 broadcast_in_dim.28.gtile
  2.0 1.3 broadcast_in_dim.26.pos
  3.3 1.5 broadcast_in_dim.29.pos_col
  4.8 76.4 %head.1 = (bf16[1024,1024]{1,0:T(8,128)(2,1)}, bf16[1024,1024]{1,0:T(8,128)(2,1)}, bf16[1024,128]{1,0:T(8,128)(2,1)}, bf16[128,1024]{1,0:T(8,128)(2,1)}, bf16[10...) custom-call(bf16[512,2048]{1,0:T(8,128)(2,1)} %bitcast.15, ...), custom_call_target="tpu_custom_call" | custom-call | tf_op jit(solution)/shard_map/head/pallas_call | solution.py:388
  81.2 152.8 %tail.1 = (bf16[512,2048]{1,0:T(8,128)(2,1)}, bf16[512,2048]{1,0:T(8,128)(2,1)}, f32[2,16,2304]{2,1,0:T(8,128)}, f32[8,128]{1,0:T(8,128)}) custom-call(bf16[1024,1024]{1,0:T(8,128)(2,1)} %get-tuple-element.24.qt, bf16[1024,1024]{1,0:T(8,128)(2,1)} %get-tuple-element.25.do_t, bf16[1024,128]{1,0:T(8,128)(2,1)} %get-tuple-element.26.k, ...), custom_call_target="tpu_custom_call" | custom-call | tf_op jit(solution)/shard_map/tail/pallas_call | solution.py:781
  234.0 1.3 dynamic-slice_bitcast_fusion
  235.3 1.0 slice_bitcast_fusion.1
  236.3 0.7 maximum_select_fusion.1
  237.0 0.6 maximum_select_fusion.3
  237.6 0.6 maximum_select_fusion.2
  238.2 0.7 maximum_select_fusion
  238.9 0.0 copy-start
  238.9 3.3 %copy.19 = bf16[1,512,2048]{2,1,0:T(8,128)(2,1)} copy(bf16[1,512,2048]{2,1,0:T(8,128)(2,1)} %bitcast.24) | data formatting | bytes 4194304
  242.2 0.0 copy-done
  242.2 1.3 copy.20
  (3 shorter events, 0.0 us)
Async XLA Ops:
  238.9 3.3 %copy-start = (bf16[512,2048]{1,0:T(8,128)(2,1)S(1)}, bf16[512,2048]{1,0:T(8,128)(2,1)}, u32[]{:S(2)}) copy-start(bf16[512,2048]{1,0:T(8,128)(2,1)} %get-tuple-element.38) | copy-start | bytes 6291460
